TPU v7x, 32 devices: a whole 2x2x4 slice. The times are simulated.
32 devices in a mesh: dom: 8 (over z, x), feat: 4 (over y, core).
Axes of the slice: x: 2, y: 2, z: 4, core: 2. Of those that a mesh axis runs over, the one named last changes fastest.
Arguments:
- items: bfloat16 [2048, 1024], P('dom', 'feat'), may hold values from -6 to 6
- self_ids: int32 [2048], P('dom'), may hold values from 0 to 2047
- neighbor_ids: int32 [2048, 50], P('dom'), may hold values from 0 to 2047
- visit_counts: int32 [2048, 50], P('dom'), may hold values from 1 to 63
- w_self: bfloat16 [1024, 1024], P('feat'), may hold values from -0.1875 to 0.1875
- w_neighbor: bfloat16 [1024, 1024], P('feat'), may hold values from -0.75 to 0.75
- bias: float32 [1024], replicated, may hold values from -3 to 3
Outputs:
- embedding: float32 [2048, 1024], P('dom', 'feat')
All inputs are finite; a program needn't handle non-finite values.
Results may differ from a plain program's by a relative error of at most 0.0018.
Values may be sent and summed in bfloat16 or wider, within the bound.
A program may use at most 64 MiB of HBM per device.

v0:
```python
import functools

import jax
import jax.numpy as jnp
from jax import lax
from jax.experimental import pallas as pl
from jax.experimental.pallas import tpu as pltpu
from jax.sharding import PartitionSpec as P

MESH = pl.DeviceIdType.MESH
LANES = 128
GROUP = 8
PARTS = 4


def kernel(
    D, F,
    items_hbm, self_hbm, ids_hbm, cnt_hbm, ws_hbm, wn_hbm, bias_hbm,
    out_ref,
    items, selfs, ids_t, cnt_t, ws, wn, bias,
    ids, cnt, key_s, lo_s, wgt_s, weights, gathered, acc,
    send_a, recv_a, send_b, recv_b, sq_out, sq_in,
    local_sem,
    up_send, up_recv, down_send, down_recv, x_send, x_recv,
    a_send_sem, a_recv_sem, b_send_sem, b_recv_sem, q_send_sem, q_recv_sem,
):
    dom, feat = lax.axis_index("dom"), lax.axis_index("feat")
    Z, H = D // 2, F // 2
    z, x = dom // 2, lax.rem(dom, 2)
    y, c = feat // 2, lax.rem(feat, 2)
    R, FC = items.shape
    nb = selfs.shape[1]
    nbr = ids.shape[1]
    share = out_ref.shape[1]
    slot = key_s.shape[1] // GROUP
    n_hi = D * R // LANES
    part = R // PARTS

    pairs = ((items_hbm, items), (ids_hbm, ids_t), (cnt_hbm, cnt_t), (self_hbm, selfs), (ws_hbm, ws), (wn_hbm, wn), (bias_hbm, bias))
    local = [pltpu.make_async_copy(a, b, local_sem.at[i]) for i, (a, b) in enumerate(pairs)]
    for copy in local:
        copy.start()

    barrier = pltpu.get_barrier_semaphore()

    def greet(d, f):
        pl.semaphore_signal(barrier, inc=1, device_id=(d, f), device_id_type=MESH)

    greet(dom + 1 - 2 * x, feat)

    @pl.when(z > 0)
    def _():
        greet(dom - 2, feat)

    @pl.when(z < Z - 1)
    def _():
        greet(dom + 2, feat)

    for k in range(1, F):
        greet(dom, lax.rem(feat + k, F))

    pl.semaphore_wait(barrier, F + (z > 0).astype(jnp.int32) + (z < Z - 1).astype(jnp.int32))
    local[0].wait()

    def rows_of(block, h):
        return pl.ds(pl.multiple_of(block * R + h * part, part), part)

    def block_copy(block, h, own, send_sem, recv_sem, target):
        dst = gathered.at[rows_of(block, h), :]
        src = items.at[pl.ds(h * part, part), :] if own else dst
        return pltpu.make_async_remote_copy(
            src_ref=src, dst_ref=dst, send_sem=send_sem, recv_sem=recv_sem,
            device_id=(target, feat), device_id_type=MESH,
        )

    def up_copy(s, h):
        i = s * PARTS + h
        return block_copy(dom - 2 * s, h, s == 0, up_send.at[i], up_recv.at[i], dom + 2)

    def down_copy(s, h):
        i = s * PARTS + h
        return block_copy(dom + 2 * s, h, s == 0, down_send.at[i], down_recv.at[i], dom - 2)

    def x_copy(step, h):
        i = (step + Z - 1) * PARTS + h
        return block_copy(dom + 2 * step, h, step == 0, x_send.at[i], x_recv.at[i], dom + 1 - 2 * x)

    def up_arrived(s, h):
        i = s * PARTS + h
        block_copy(dom - 2 * (s + 1), h, False, up_send.at[i], up_recv.at[i], dom).wait_recv()

    def down_arrived(s, h):
        i = s * PARTS + h
        block_copy(dom + 2 * (s + 1), h, False, down_send.at[i], down_recv.at[i], dom).wait_recv()

    def x_arrived(step, h):
        i = (step + Z - 1) * PARTS + h
        block_copy(dom + 1 - 2 * x + 2 * step, h, False, x_send.at[i], x_recv.at[i], dom).wait_recv()

    for h in range(PARTS):
        @pl.when(z < Z - 1)
        def _():
            up_copy(0, h).start()

        @pl.when(z > 0)
        def _():
            down_copy(0, h).start()

        x_copy(0, h).start()

    def forward(s, h):
        @pl.when(z > s)
        def _():
            up_arrived(s, h)

            @pl.when(z < Z - 1)
            def _():
                up_copy(s + 1, h).start()

            x_copy(-(s + 1), h).start()

        @pl.when(z < Z - 1 - s)
        def _():
            down_arrived(s, h)

            @pl.when(z > 0)
            def _():
                down_copy(s + 1, h).start()

            x_copy(s + 1, h).start()

    for copy in local[1:4]:
        copy.wait()
    ids[...] = jnp.transpose(ids_t[...])
    cnt[...] = jnp.transpose(cnt_t[...])
    wgt_s[...] = jnp.zeros_like(wgt_s)
    lo_s[...] = jnp.zeros_like(lo_s)
    key_s[...] = jnp.zeros_like(key_s)
    for j in range(GROUP):
        ids_j = ids[pl.ds(j, nb // GROUP, stride=GROUP), :]
        at = slice(j * slot, j * slot + nbr)
        key_s[:, at] = (ids_j // LANES) * GROUP + j
        lo_s[:, at] = lax.rem(ids_j, LANES)
        wgt_s[:, at] = cnt[pl.ds(j, nb // GROUP, stride=GROUP), :].astype(jnp.float32)

    K = key_s.shape[1]

    def half_group(g):
        key = key_s[pl.ds(g, 1), :]
        low = lo_s[pl.ds(g, 1), :]
        wgt = wgt_s[pl.ds(g, 1), :]
        left = jnp.where(lax.broadcasted_iota(jnp.int32, (n_hi * GROUP, K), 0) == key, wgt, 0.0)
        right = jnp.where(lax.broadcasted_iota(jnp.int32, (LANES, K), 0) == low, 1.0, 0.0)
        return lax.dot_general(
            left.astype(jnp.bfloat16), right.astype(jnp.bfloat16),
            (((1,), (1,)), ((), ())), preferred_element_type=jnp.float32,
        )

    def build(it, carry):
        first, second = half_group(it * 2), half_group(it * 2 + 1)
        at = pl.ds(pl.multiple_of(nb + it * 2 * GROUP, 2 * GROUP), 2 * GROUP)
        for hi in range(n_hi):
            rows = slice(hi * GROUP, (hi + 1) * GROUP)
            tile = jnp.concatenate([first[rows], second[rows]], axis=0)
            weights[at, hi * LANES:(hi + 1) * LANES] = tile.astype(jnp.bfloat16)
        return carry

    def build_pair(it, carry):
        return build(it * 2 + 1, build(it * 2, carry))

    pairs_here = nb // (4 * GROUP)
    for h in range(PARTS):
        lax.fori_loop(pairs_here * h // PARTS, pairs_here * (h + 1) // PARTS, build_pair, 0)
        forward(0, h)
    self_col = jnp.transpose(jnp.broadcast_to(selfs[...], (LANES, nb)))
    lane = lax.broadcasted_iota(jnp.int32, (nb, LANES), 1)
    for hi in range(n_hi):
        hit = jnp.where(self_col == lane + hi * LANES, 1.0, 0.0)
        weights[0:nb, hi * LANES:(hi + 1) * LANES] = hit.astype(jnp.bfloat16)
    total = jnp.sum(cnt[...].astype(jnp.float32), axis=1, keepdims=True)

    def columns(block):
        return weights[:, pl.ds(pl.multiple_of(block * R, R), R)]

    def add(block):
        rows = pl.ds(pl.multiple_of(block * R, R), R)
        acc[...] += jnp.dot(columns(block), gathered[rows, :], preferred_element_type=jnp.float32)

    def add_line(step, z_now, wait):
        @pl.when((z_now + step >= 0) & (z_now + step < Z))
        def _():
            if wait:
                for h in range(PARTS):
                    x_arrived(step, h)
                add(dom + 1 - 2 * x + 2 * step)
            else:
                add(dom + 2 * step)

    acc[...] = jnp.dot(columns(dom), items[...], preferred_element_type=jnp.float32)
    add_line(0, z, True)
    for s in range(Z - 1):
        if s > 0:
            for h in range(PARTS):
                forward(s, h)
        for step in (-(s + 1), s + 1):
            add_line(step, z, False)
        if s > 0:
            for step in (-s, s):
                add_line(step, z, True)
    for step in (-(Z - 1), Z - 1):
        add_line(step, z, True)

    own = acc[0:nb, :].astype(jnp.bfloat16)
    pooled = (acc[nb:2 * nb, :] / total).astype(jnp.bfloat16)
    local[4].wait()
    local[5].wait()
    local[6].wait()

    def project(yy, cc):
        cols = pl.ds(pl.multiple_of((yy * 2 + cc) * share, share), share)
        return jnp.dot(own, ws[:, cols], preferred_element_type=jnp.float32) + jnp.dot(
            pooled, wn[:, cols], preferred_element_type=jnp.float32
        )

    def a_copy(k):
        return pltpu.make_async_remote_copy(
            src_ref=send_a.at[k], dst_ref=recv_a.at[k], send_sem=a_send_sem.at[k], recv_sem=a_recv_sem.at[k],
            device_id=(dom, feat + 1 - 2 * c), device_id_type=MESH,
        )

    def b_copy(k):
        return pltpu.make_async_remote_copy(
            src_ref=send_b.at[k], dst_ref=recv_b.at[k], send_sem=b_send_sem.at[k], recv_sem=b_recv_sem.at[k],
            device_id=(dom, lax.rem(y + k + 1, H) * 2 + c), device_id_type=MESH,
        )

    for k in range(H):
        send_a[k] = project(lax.rem(y + k + 1, H), 1 - c)
        a_copy(k).start()
    mine = None
    for k in range(H):
        here = project(lax.rem(y + k + 1, H), c)
        a_copy(k).wait_recv()
        summed = here + recv_a[k]
        if k < H - 1:
            send_b[k] = summed.astype(jnp.bfloat16)
            b_copy(k).start()
        else:
            mine = summed + bias[:, pl.ds(pl.multiple_of(feat * share, share), share)]
    for k in range(H - 1):
        b_copy(k).wait_recv()
        mine = mine + recv_b[k].astype(jnp.float32)
    hidden = jnp.maximum(mine, 0.0)
    squares = jnp.sum(hidden * hidden, axis=1, keepdims=True)
    row = jnp.transpose(jnp.broadcast_to(squares, (nb, LANES)))[0:GROUP, :]
    sq_out[...] = row

    def q_copy(k):
        return pltpu.make_async_remote_copy(
            src_ref=sq_out, dst_ref=sq_in.at[k - 1], send_sem=q_send_sem.at[k - 1], recv_sem=q_recv_sem.at[k - 1],
            device_id=(dom, lax.rem(feat + k, F)), device_id_type=MESH,
        )

    for k in range(1, F):
        q_copy(k).start()
    for k in range(1, F):
        q_copy(k).wait_recv()
        row = row + sq_in[k - 1]
    scale = lax.rsqrt(row / (share * F) + 1e-06)[0:1, :]
    column = jnp.transpose(jnp.broadcast_to(scale, (LANES, nb)))
    for i in range(share // LANES):
        at = slice(i * LANES, (i + 1) * LANES)
        out_ref[:, at] = hidden[:, at] * column

    for s in range(Z - 1):
        for h in range(PARTS):
            @pl.when((z < Z - 1) & (z >= s))
            def _():
                up_copy(s, h).wait_send()

            @pl.when((z > 0) & (z < Z - s))
            def _():
                down_copy(s, h).wait_send()
    for step in range(-(Z - 1), Z):
        @pl.when((z + step >= 0) & (z + step < Z))
        def _():
            for h in range(PARTS):
                x_copy(step, h).wait_send()
    for k in range(H):
        a_copy(k).wait_send()
    for k in range(H - 1):
        b_copy(k).wait_send()
    for k in range(1, F):
        q_copy(k).wait_send()


def shards(D, F, items, self_ids, neighbor_ids, visit_counts, w_self, w_neighbor, bias):
    R, FC = items.shape
    nb, nbr = neighbor_ids.shape
    out = bias.shape[0]
    share = out // F
    slot = 1 << (nbr - 1).bit_length()
    Z, H = D // 2, F // 2
    lines = (Z - 1) * PARTS
    f32, bf16, i32 = jnp.float32, jnp.bfloat16, jnp.int32
    dma = pltpu.SemaphoreType.DMA
    return pl.pallas_call(
        functools.partial(kernel, D, F),
        out_shape=pltpu.VMEM((nb, share), f32),
        in_specs=[pl.BlockSpec(memory_space=pl.ANY)] * 7,
        out_specs=pl.BlockSpec(memory_space=pltpu.VMEM),
        scratch_shapes=[
            pltpu.VMEM((R, FC), bf16),
            pltpu.VMEM((1, nb), i32),
            pltpu.VMEM((nbr, nb), i32),
            pltpu.VMEM((nbr, nb), i32),
            pltpu.VMEM((FC, out), bf16),
            pltpu.VMEM((FC, out), bf16),
            pltpu.VMEM((1, out), f32),
            pltpu.VMEM((nb, nbr), i32),
            pltpu.VMEM((nb, nbr), i32),
            pltpu.VMEM((nb // GROUP, GROUP * slot), i32),
            pltpu.VMEM((nb // GROUP, GROUP * slot), i32),
            pltpu.VMEM((nb // GROUP, GROUP * slot), f32),
            pltpu.VMEM((2 * nb, D * R), bf16),
            pltpu.VMEM((D * R, FC), bf16),
            pltpu.VMEM((2 * nb, FC), f32),
            pltpu.VMEM((H, nb, share), f32),
            pltpu.VMEM((H, nb, share), f32),
            pltpu.VMEM((H - 1, nb, share), bf16),
            pltpu.VMEM((H - 1, nb, share), bf16),
            pltpu.VMEM((GROUP, nb), f32),
            pltpu.VMEM((F - 1, GROUP, nb), f32),
            dma((7,)),
            dma((lines,)), dma((lines,)), dma((lines,)), dma((lines,)),
            dma(((2 * Z - 1) * PARTS,)), dma(((2 * Z - 1) * PARTS,)),
            dma((H,)), dma((H,)), dma((H - 1,)), dma((H - 1,)), dma((F - 1,)), dma((F - 1,)),
        ],
        compiler_params=pltpu.CompilerParams(collective_id=0, has_side_effects=True),
    )(items, self_ids.reshape(1, nb), neighbor_ids.T, visit_counts.T, w_self, w_neighbor, bias.reshape(1, out))


def solution(mesh):
    placed = (
        P("dom", "feat"),
        P("dom"),
        P("dom", None),
        P("dom", None),
        P("feat", None),
        P("feat", None),
        P(),
    )
    return jax.shard_map(
        functools.partial(shards, mesh.shape["dom"], mesh.shape["feat"]),
        mesh=mesh, in_specs=placed, out_specs=P("dom", "feat"), check_vma=False,
    )
```

profile of v0, /device:TPU:0, one launch (start us, length us, event | category | flops | bytes accessed | tf_op | source)
XLA Modules:
  0.0 30.2 jit_solution(289520428556035324)
XLA Ops:
  0.0 29.4 %shard_map.73 = f32[256,256]{1,0:T(8,128)S(1)} custom-call(bf16[256,256]{1,0:T(8,128)(2,1)} %items_hbm.1, s32[1,256]{1,0:T(1,128)} %bitcast.7, s32[50,256]{1,0:T(8,128)} %bitcast.4, s32[50,256]{1,0:T(8,128)} %bitcast.5, bf16[256,1024]{1,0:T(8,128)(2,1)} %ws_hbm.1, bf16[256,1024]{1,0:T(8,128)(2,1)} %wn_hbm.1, f32[1,1024]{1,0:T(1,128)} %bitcast.6), custom_call_target="tpu_custom_call" | custom-call | tf_op jit(solution)/shard_map/pallas_call | solution.py:307
  29.5 0.7 %copy.9 = f32[256,256]{1,0:T(8,128)} copy(f32[256,256]{1,0:T(8,128)S(1)} %shard_map.73) | data formatting | bytes 524288
where the time goes:
time: 30.3 us; the launch traced here: 30.2 us
  Pallas kernels  29.4 us (97%)
  local copies, waits for them, and re-layouts  0.71 us (2%)
    pallas_call x1, Pallas kernels, shards(): pl.pallas_call(functools.partial(kernel, D, F), out_shape=pltpu.VMEM((nb,...  29.4 us
    unnamed x1, local copies, waits for them, and re-layouts  0.71 us

commit v1 on v0

v1 whole, which is shorter than its diff:
```python
import functools

import jax
import jax.numpy as jnp
from jax import lax
from jax.experimental import pallas as pl
from jax.experimental.pallas import tpu as pltpu
from jax.sharding import PartitionSpec as P

MESH = pl.DeviceIdType.MESH
LANES = 128
GROUP = 8
PARTS = 4
SIDE = 2
CHUNKS = 2
PIECES = 2


def kernel(
    D, F,
    items_hbm, self_hbm, ids_hbm, cnt_hbm, ws_hbm, wn_hbm, bias_hbm,
    out_ref,
    selfs, ids_t, cnt_t, w_all, bias,
    ids, cnt, key_s, lo_s, wgt_s, weights, gathered, acc, both,
    send_a, recv_a, send_b, recv_b, sq_out, sq_in,
    local_sem,
    up_send, down_send, line_recv, x_send, x_recv,
    a_send_sem, a_recv_sem, b_send_sem, b_recv_sem, q_send_sem, q_recv_sem,
    side_send, side_recv, ready_up, ready_x, ready_feat,
):
    dom, feat = lax.axis_index("dom"), lax.axis_index("feat")
    Z, H = D // 2, F // 2
    z, x = dom // 2, lax.rem(dom, 2)
    y, c = feat // 2, lax.rem(feat, 2)
    R, FC = items_hbm.shape
    nb = selfs.shape[1]
    nbr = ids.shape[1]
    share = out_ref.shape[1]
    slot = key_s.shape[1] // GROUP
    n_hi = D * R // LANES
    part = R // PARTS
    other = dom + 1 - 2 * x

    barrier = pltpu.get_barrier_semaphore()
    line = [k for k in (1, 2) if k < Z]
    toward = 1 - 2 * lax.rem(z, 2)

    def signal(sem, d, f):
        pl.semaphore_signal(sem, inc=1, device_id=(d, f), device_id_type=MESH)

    for k in line:
        pl.when(z + k < Z)(functools.partial(signal, barrier, dom + 2 * k, feat))
    pl.when(x == 0)(functools.partial(signal, barrier, other, feat))
    for k in range(1, F):
        pl.when(feat + k < F)(functools.partial(signal, barrier, dom, feat + k))

    mine = pl.ds(pl.multiple_of(dom * R, R), R)
    pairs = (
        (ids_hbm, ids_t), (cnt_hbm, cnt_t), (self_hbm, selfs), (items_hbm, gathered.at[mine, :]),
        (ws_hbm, w_all.at[0:FC]), (wn_hbm, w_all.at[FC:2 * FC]),
    )
    local = [pltpu.make_async_copy(a, b, local_sem.at[min(i, 4)]) for i, (a, b) in enumerate(pairs)]
    for copy in local[0:3]:
        copy.start()
    lower = x + feat
    for k in line:
        lower = lower + (z >= k).astype(jnp.int32)
    pl.when(lower > 0)(lambda: pl.semaphore_wait(barrier, lower))

    def rows_of(block, h, n=1):
        return pl.ds(pl.multiple_of(block * R + h * part, part), n * part)

    def block_copy(block, h, n, own, send_sem, recv_sem, target):
        dst = gathered.at[rows_of(block, h, n), :]
        src = items_hbm.at[rows_of(0, h, n), :] if own else dst
        return pltpu.make_async_remote_copy(
            src_ref=src, dst_ref=dst, send_sem=send_sem, recv_sem=recv_sem,
            device_id=(target, feat), device_id_type=MESH,
        )

    def line_copy(s, h, sign, send, n=1):
        own = s < 2
        block = dom if own else dom - 2 * sign * s
        target = dom + 2 * sign * (s + 1 if own else 1)
        return block_copy(block, h, n, own, send.at[s], line_recv.at[(block // 2) * PARTS + h], target)

    def up_copy(s, h, n=1):
        return line_copy(s, h, 1, up_send, n)

    def down_copy(s, h, n=1):
        return line_copy(s, h, -1, down_send, n)

    def line_arrived(step, h):
        block = dom + 2 * step
        block_copy(block, h, 1, False, up_send.at[0], line_recv.at[(block // 2) * PARTS + h], dom).wait_recv()

    def x_copy(step, h, n=1):
        own = isinstance(step, int) and step == 0
        return block_copy(dom + 2 * step, h, n, own, x_send.at[z + step], x_recv.at[z + step], other)

    def x_arrived(step, n=PARTS):
        block_copy(other + 2 * step, 0, n, False, x_send.at[z + step], x_recv.at[z + step], dom).wait_recv()

    def side_copy(h, n=1):
        return block_copy(other, h, n, False, side_send, side_recv, dom + 2 * toward)

    inner = (z > 0) & (z < Z - 1)

    def own_down(s):
        for h in range(PARTS):
            down_copy(s, h).start()

    for k in reversed(line):
        pl.when(inner & (z >= k))(functools.partial(own_down, k - 1))
    for k in line:
        pl.when(z == Z - 1)(functools.partial(own_down, k - 1))

    def across():
        for h in range(PARTS):
            x_copy(0, h).start()

    pl.when(x == 1)(across)
    for k in line:
        pl.when(z >= k)(functools.partial(signal, ready_up.at[k - 1], dom - 2 * k, feat))
    pl.when(x == 1)(functools.partial(signal, ready_x, other, feat))
    for k in range(1, F):
        pl.when(feat >= k)(functools.partial(signal, ready_feat, dom, feat - k))
    for copy in local[3:]:
        copy.start()
    bias_load = pltpu.make_async_copy(bias_hbm, bias, local_sem.at[5])
    bias_load.start()

    def over_x(s, h, sign):
        if s > 0:
            x_copy(sign * (s + 1), h).start()
        else:
            @pl.when((h < SIDE) | (toward != sign))
            def _():
                x_copy(sign, h).start()

    def from_above(s, h):
        @pl.when(z < Z - 1 - s)
        def _():
            line_arrived(s + 1, h)
            if 0 < s < Z - 2:
                pl.when(z > 0)(lambda: down_copy(s + 1, h).start())
            over_x(s, h, 1)

    def from_below(s, h):
        @pl.when(z > s)
        def _():
            line_arrived(-(s + 1), h)
            if 0 < s < Z - 2:
                pl.when(z < Z - 1)(lambda: up_copy(s + 1, h).start())
            over_x(s, h, -1)

    def forward(s, h):
        pl.when(z < Z // 2)(lambda: from_below(s, h))
        from_above(s, h)
        pl.when(z >= Z // 2)(lambda: from_below(s, h))

    def sides():
        x_arrived(0)
        for h in range(SIDE, PARTS):
            side_copy(h).start()

    for copy in local[0:3]:
        copy.wait()
    ids[...] = jnp.transpose(ids_t[...])
    cnt[...] = jnp.transpose(cnt_t[...])
    wgt_s[...] = jnp.zeros_like(wgt_s)
    lo_s[...] = jnp.zeros_like(lo_s)
    key_s[...] = jnp.zeros_like(key_s)
    for j in range(GROUP):
        ids_j = ids[pl.ds(j, nb // GROUP, stride=GROUP), :]
        at = slice(j * slot, j * slot + nbr)
        key_s[:, at] = (ids_j // LANES) * GROUP + j
        lo_s[:, at] = lax.rem(ids_j, LANES)
        wgt_s[:, at] = cnt[pl.ds(j, nb // GROUP, stride=GROUP), :].astype(jnp.float32)

    K = key_s.shape[1]

    def half_group(g):
        key = key_s[pl.ds(g, 1), :]
        low = lo_s[pl.ds(g, 1), :]
        wgt = wgt_s[pl.ds(g, 1), :]
        left = jnp.where(lax.broadcasted_iota(jnp.int32, (n_hi * GROUP, K), 0) == key, wgt, 0.0)
        right = jnp.where(lax.broadcasted_iota(jnp.int32, (LANES, K), 0) == low, 1.0, 0.0)
        return lax.dot_general(
            left.astype(jnp.bfloat16), right.astype(jnp.bfloat16),
            (((1,), (1,)), ((), ())), preferred_element_type=jnp.float32,
        )

    def build(it, carry):
        first, second = half_group(it * 2), half_group(it * 2 + 1)
        at = pl.ds(pl.multiple_of(nb + it * 2 * GROUP, 2 * GROUP), 2 * GROUP)
        for hi in range(n_hi):
            rows = slice(hi * GROUP, (hi + 1) * GROUP)
            tile = jnp.concatenate([first[rows], second[rows]], axis=0)
            weights[at, hi * LANES:(hi + 1) * LANES] = tile.astype(jnp.bfloat16)
        return carry

    def build_pair(it, carry):
        return build(it * 2 + 1, build(it * 2, carry))

    self_col = jnp.transpose(jnp.broadcast_to(selfs[...], (LANES, nb)))
    lane = lax.broadcasted_iota(jnp.int32, (nb, LANES), 1)
    inverse = 1.0 / jnp.sum(cnt[...].astype(jnp.float32), axis=1, keepdims=True)

    @pl.when(x == 0)
    def _():
        pl.semaphore_wait(ready_x, 1)
        across()

    def own_up(k):
        pl.semaphore_wait(ready_up.at[k - 1], 1)
        for h in range(PARTS):
            up_copy(k - 1, h).start()

    for k in reversed(line):
        pl.when(inner & (z + k < Z))(functools.partial(own_up, k))
    for k in line:
        pl.when(z == 0)(functools.partial(own_up, k))

    units = nb // (4 * GROUP)
    early = units - PARTS * (-(-units // (2 * PARTS)))
    late = units - early
    lax.fori_loop(0, early, build_pair, 0)
    for h in range(SIDE):
        pl.when(z == 0)(functools.partial(from_above, 0, h))
        pl.when(z == Z - 1)(functools.partial(from_below, 0, h))

    def slot(h, carry):
        carry = lax.fori_loop(early + late * h // PARTS, early + late * (h + 1) // PARTS, build_pair, carry)
        forward(1, h)
        return carry

    lax.fori_loop(0, PARTS, slot, 0)
    sides()

    def self_weights():
        for hi in range(n_hi):
            hit = jnp.where(self_col == lane + hi * LANES, 1.0, 0.0)
            weights[0:nb, hi * LANES:(hi + 1) * LANES] = hit.astype(jnp.bfloat16)

    def add(block, low, high):
        rows = pl.ds(pl.multiple_of(block * R + low * part, part), (high - low) * part)
        at = pl.ds(pl.multiple_of(block * R + low * part, LANES), (high - low) * part)
        acc[...] += jnp.dot(weights[:, at], gathered[rows, :], preferred_element_type=jnp.float32)

    def if_there(step, work):
        pl.when((z + step >= 0) & (z + step < Z))(work)

    def add_z(step):
        def work():
            add(dom + 2 * step, 0, PARTS)
        if_there(step, work)

    def add_x(step):
        def work():
            x_arrived(step)
            add(other + 2 * step, 0, PARTS)
        if_there(step, work)

    def add_pair():
        x_arrived(toward, SIDE)
        block_copy(other + 2 * toward, SIDE, PARTS - SIDE, False, side_send, side_recv, dom).wait_recv()
        add(other + 2 * toward, 0, PARTS)

    def add_next():
        def work():
            x_arrived(-toward)
            add(other - 2 * toward, 0, PARTS)
        pl.when((z - toward >= 0) & (z - toward < Z))(work)

    def both_ways(work, s):
        work(-s)
        work(s)

    def first_dots():
        local[3].wait()
        acc[...] = jnp.dot(weights[:, mine], gathered[mine, :], preferred_element_type=jnp.float32)
        add(other, 0, PARTS)

    todo = [self_weights, first_dots, functools.partial(both_ways, add_z, 2)]
    for h in range(PARTS):
        if h < len(todo):
            todo[h]()
        if h < SIDE:
            pl.when(inner)(functools.partial(forward, 0, h))
        else:
            forward(0, h)
    for s in range(2, Z - 1):
        todo = [functools.partial(both_ways, add_z, 1)] if s == 2 else [functools.partial(both_ways, add_z, s)]
        for h in range(PARTS):
            if h < len(todo):
                todo[h]()
            forward(s, h)
    both_ways(add_z, Z - 1)
    both_ways(add_x, 2)
    add_pair()
    add_next()
    for s in range(3, Z):
        both_ways(add_x, s)

    pltpu.make_async_copy(w_all, w_all, local_sem.at[4]).wait()
    bias_load.wait()
    pl.when(feat < F - 1)(lambda: pl.semaphore_wait(ready_feat, F - 1 - feat))
    both[:, 0:FC] = acc[0:nb, :].astype(jnp.bfloat16)
    both[:, FC:2 * FC] = (acc[nb:2 * nb, :] * inverse).astype(jnp.bfloat16)
    tall = nb // CHUNKS
    short = tall // PIECES

    def chunk(r):
        return pl.ds(r * tall, tall)

    def project(r, yy, cc):
        cols = pl.ds(pl.multiple_of((yy * 2 + cc) * share, share), share)
        return jnp.dot(both[chunk(r), :], w_all[:, cols], preferred_element_type=jnp.float32)

    def a_copy(k, r):
        i = k * CHUNKS + r
        return pltpu.make_async_remote_copy(
            src_ref=send_a.at[k, chunk(r)], dst_ref=recv_a.at[k, chunk(r)],
            send_sem=a_send_sem, recv_sem=a_recv_sem.at[i],
            device_id=(dom, feat + 1 - 2 * c), device_id_type=MESH,
        )

    def b_copy(k, p):
        i = k * CHUNKS * PIECES + p
        at = pl.ds(p * short, short)
        return pltpu.make_async_remote_copy(
            src_ref=send_b.at[k, at], dst_ref=recv_b.at[k, at], send_sem=b_send_sem, recv_sem=b_recv_sem.at[i],
            device_id=(dom, lax.rem(y + k + 1, H) * 2 + c), device_id_type=MESH,
        )

    def q_copy(k, r):
        return pltpu.make_async_remote_copy(
            src_ref=sq_out.at[r], dst_ref=sq_in.at[r, k - 1], send_sem=q_send_sem, recv_sem=q_recv_sem.at[r],
            device_id=(dom, lax.rem(feat + k, F)), device_id_type=MESH,
        )

    def all_of(ref, send_sem, recv_sem):
        return pltpu.make_async_remote_copy(
            src_ref=ref, dst_ref=ref, send_sem=send_sem, recv_sem=recv_sem, device_id=(dom, feat), device_id_type=MESH,
        )

    for k in range(H):
        yy = lax.rem(y + k + 1, H)
        for r in range(CHUNKS):
            send_a[k, chunk(r)] = project(r, yy, 1 - c)
            a_copy(k, r).start()
        for r in range(CHUNKS):
            here = project(r, yy, c)
            a_copy(k, r).wait_recv()
            summed = here + recv_a[k, chunk(r)]
            if k < H - 1:
                send_b[k, chunk(r)] = summed.astype(jnp.bfloat16)
                for p in range(r * PIECES, (r + 1) * PIECES):
                    b_copy(k, p).start()
            else:
                out_ref[chunk(r), :] = summed + bias[:, pl.ds(pl.multiple_of(feat * share, share), share)]

    for s in range(Z - 1):
        pl.when((z + s + 1 < Z) if s < 2 else (z < Z - 1) & (z >= s))(lambda: up_copy(s, 0, PARTS).wait_send())
        pl.when((z > s) if s < 2 else (z > 0) & (z + s < Z))(lambda: down_copy(s, 0, PARTS).wait_send())
    side_copy(SIDE, PARTS - SIDE).wait_send()
    x_copy(0, 0, PARTS).wait_send()
    x_copy(toward, 0, SIDE).wait_send()
    pl.when((z - toward >= 0) & (z - toward < Z))(lambda: x_copy(-toward, 0, PARTS).wait_send())
    for step in range(2, Z):
        pl.when(z + step < Z)(lambda: x_copy(step, 0, PARTS).wait_send())
        pl.when(z >= step)(lambda: x_copy(-step, 0, PARTS).wait_send())

    for r in range(CHUNKS):
        squares = []
        for p in range(r * PIECES, (r + 1) * PIECES):
            at = pl.ds(p * short, short)
            total = out_ref[at, :]
            for k in range(H - 1):
                b_copy(k, p).wait_recv()
                total = total + recv_b[k, at].astype(jnp.float32)
            hidden = jnp.maximum(total, 0.0)
            out_ref[at, :] = hidden
            square = hidden * hidden
            folded = square[:, 0:LANES]
            for i in range(1, share // LANES):
                folded = folded + square[:, i * LANES:(i + 1) * LANES]
            squares.append(folded)
        turned = jnp.transpose(jnp.concatenate(squares, axis=0))
        row = jnp.sum(turned, axis=0, keepdims=True)
        sq_out[r] = jnp.broadcast_to(row, (GROUP, tall))
        for k in range(1, F):
            q_copy(k, r).start()

    for r in range(CHUNKS):
        all_of(sq_in.at[r], q_send_sem, q_recv_sem.at[r]).wait_recv()
        row = sq_out[r]
        for k in range(1, F):
            row = row + sq_in[r, k - 1]
        scale = lax.rsqrt(row / (share * F) + 1e-06)[0:1, :]
        column = jnp.transpose(jnp.broadcast_to(scale, (LANES, tall)))
        for i in range(share // LANES):
            at = slice(i * LANES, (i + 1) * LANES)
            out_ref[chunk(r), at] = out_ref[chunk(r), at] * column

    all_of(send_a, a_send_sem, a_recv_sem.at[0]).wait_send()
    all_of(send_b, b_send_sem, b_recv_sem.at[0]).wait_send()
    all_of(sq_in, q_send_sem, q_recv_sem.at[0]).wait_send()


def shards(D, F, items, self_ids, neighbor_ids, visit_counts, w_self, w_neighbor, bias):
    R, FC = items.shape
    nb, nbr = neighbor_ids.shape
    out = bias.shape[0]
    share = out // F
    slot = 1 << (nbr - 1).bit_length()
    Z, H = D // 2, F // 2
    f32, bf16, i32 = jnp.float32, jnp.bfloat16, jnp.int32
    dma, flag = pltpu.SemaphoreType.DMA, pltpu.SemaphoreType.REGULAR
    return pl.pallas_call(
        functools.partial(kernel, D, F),
        out_shape=pltpu.VMEM((nb, share), f32),
        in_specs=[pl.BlockSpec(memory_space=pl.ANY)] * 7,
        out_specs=pl.BlockSpec(memory_space=pltpu.VMEM),
        scratch_shapes=[
            pltpu.VMEM((1, nb), i32),
            pltpu.VMEM((nbr, nb), i32),
            pltpu.VMEM((nbr, nb), i32),
            pltpu.VMEM((2 * FC, out), bf16),
            pltpu.VMEM((1, out), f32),
            pltpu.VMEM((nb, nbr), i32),
            pltpu.VMEM((nb, nbr), i32),
            pltpu.VMEM((nb // GROUP, GROUP * slot), i32),
            pltpu.VMEM((nb // GROUP, GROUP * slot), i32),
            pltpu.VMEM((nb // GROUP, GROUP * slot), f32),
            pltpu.VMEM((2 * nb, D * R), bf16),
            pltpu.VMEM((D * R, FC), bf16),
            pltpu.VMEM((2 * nb, FC), f32),
            pltpu.VMEM((nb, 2 * FC), bf16),
            pltpu.VMEM((H, nb, share), f32),
            pltpu.VMEM((H, nb, share), f32),
            pltpu.VMEM((H - 1, nb, share), bf16),
            pltpu.VMEM((H - 1, nb, share), bf16),
            pltpu.VMEM((CHUNKS, GROUP, nb // CHUNKS), f32),
            pltpu.VMEM((CHUNKS, F - 1, GROUP, nb // CHUNKS), f32),
            dma((6,)),
            dma((Z - 1,)), dma((Z - 1,)), dma((Z * PARTS,)), dma((Z,)), dma((Z,)),
            dma, dma((H * CHUNKS,)), dma, dma(((H - 1) * CHUNKS * PIECES,)), dma, dma((CHUNKS,)),
            dma, dma, flag((2,)), flag, flag,
        ],
        compiler_params=pltpu.CompilerParams(collective_id=0, has_side_effects=True),
    )(items, self_ids.reshape(1, nb), neighbor_ids.T, visit_counts.T, w_self, w_neighbor, bias.reshape(1, out))


def solution(mesh):
    placed = (
        P("dom", "feat"),
        P("dom"),
        P("dom", None),
        P("dom", None),
        P("feat", None),
        P("feat", None),
        P(),
    )
    return jax.shard_map(
        functools.partial(shards, mesh.shape["dom"], mesh.shape["feat"]),
        mesh=mesh, in_specs=placed, out_specs=P("dom", "feat"), check_vma=False,
    )
```

time: 30.3 us -> 29 us (0.957)
  Pallas kernels: 29.4 us -> 28.1 us
    pallas_call x1, Pallas kernels: 29.4 us -> 28.1 us  [shards(): pl.pallas_call(functools.partial(kernel, D, F), out_shape=pltpu.VMEM((nb,...]
where the time goes in v1:
time: 29 us; the launch traced here: 28.8 us
  Pallas kernels  28.1 us (97%)
  local copies, waits for them, and re-layouts  0.71 us (2%)
    pallas_call x1, Pallas kernels, shards(): pl.pallas_call(functools.partial(kernel, D, F), out_shape=pltpu.VMEM((nb,...  28.1 us
    unnamed x1, local copies, waits for them, and re-layouts  0.71 us

profile of v1, /device:TPU:0, one launch (start us, length us, event | category | flops | bytes accessed | tf_op | source)
XLA Modules:
  0.0 28.8 jit_solution(5571836502446906606)
XLA Ops:
  0.0 28.1 %shard_map.73 = f32[256,256]{1,0:T(8,128)S(1)} custom-call(bf16[256,256]{1,0:T(8,128)(2,1)} %items_hbm.1, s32[1,256]{1,0:T(1,128)} %bitcast.7, s32[50,256]{1,0:T(8,128)} %bitcast.4, s32[50,256]{1,0:T(8,128)} %bitcast.5, bf16[256,1024]{1,0:T(8,128)(2,1)} %ws_hbm.1, bf16[256,1024]{1,0:T(8,128)(2,1)} %wn_hbm.1, f32[1,1024]{1,0:T(1,128)} %bitcast.6), custom_call_target="tpu_custom_call" | custom-call | tf_op jit(solution)/shard_map/pallas_call | solution.py:421
  28.1 0.7 %copy.9 = f32[256,256]{1,0:T(8,128)} copy(f32[256,256]{1,0:T(8,128)S(1)} %shard_map.73) | data formatting | bytes 524288

commit v2 on v1

--- a/solution.py
+++ b/solution.py
@@ -43,7 +43,8 @@
 
     barrier = pltpu.get_barrier_semaphore()
     line = [k for k in (1, 2) if k < Z]
-    toward = 1 - 2 * lax.rem(z, 2)
+    lower, upper = z < Z // 2, z >= Z // 2
+    inward = jnp.where(lower, 1, -1)
 
     def signal(sem, d, f):
         pl.semaphore_signal(sem, inc=1, device_id=(d, f), device_id_type=MESH)
@@ -62,10 +63,10 @@
     local = [pltpu.make_async_copy(a, b, local_sem.at[min(i, 4)]) for i, (a, b) in enumerate(pairs)]
     for copy in local[0:3]:
         copy.start()
-    lower = x + feat
+    below = x + feat
     for k in line:
-        lower = lower + (z >= k).astype(jnp.int32)
-    pl.when(lower > 0)(lambda: pl.semaphore_wait(barrier, lower))
+        below = below + (z >= k).astype(jnp.int32)
+    pl.when(below > 0)(lambda: pl.semaphore_wait(barrier, below))
 
     def rows_of(block, h, n=1):
         return pl.ds(pl.multiple_of(block * R + h * part, part), n * part)
@@ -95,16 +96,20 @@
         block_copy(block, h, 1, False, up_send.at[0], line_recv.at[(block // 2) * PARTS + h], dom).wait_recv()
 
     def x_copy(step, h, n=1):
-        own = isinstance(step, int) and step == 0
-        return block_copy(dom + 2 * step, h, n, own, x_send.at[z + step], x_recv.at[z + step], other)
-
-    def x_arrived(step, n=PARTS):
-        block_copy(other + 2 * step, 0, n, False, x_send.at[z + step], x_recv.at[z + step], dom).wait_recv()
-
-    def side_copy(h, n=1):
-        return block_copy(other, h, n, False, side_send, side_recv, dom + 2 * toward)
-
-    inner = (z > 0) & (z < Z - 1)
+        at = Z if step == 0 and h >= SIDE else z + step
+        return block_copy(dom + 2 * step, h, n, step == 0, x_send.at[z + step], x_recv.at[at], other)
+
+    def x_arrived(step, h, n):
+        at = Z if h >= SIDE else z + step
+        block_copy(other + 2 * step, h, n, False, x_send.at[z + step], x_recv.at[at], dom).wait_recv()
+
+    def side_down(target):
+        return block_copy(D - 1 - x, SIDE, PARTS - SIDE, False, side_send.at[0], side_recv.at[0], target)
+
+    def side_up(target):
+        return block_copy(1 - x, SIDE, PARTS - SIDE, False, side_send.at[1], side_recv.at[1], target)
+
+    inner, outer = (z > 0) & (z < Z - 1), (z == 0) | (z == Z - 1)
 
     def own_down(s):
         for h in range(PARTS):
@@ -112,11 +117,10 @@
 
     for k in reversed(line):
         pl.when(inner & (z >= k))(functools.partial(own_down, k - 1))
-    for k in line:
-        pl.when(z == Z - 1)(functools.partial(own_down, k - 1))
+    pl.when(z == Z - 1)(functools.partial(own_down, line[-1] - 1))
 
     def across():
-        for h in range(PARTS):
+        for h in [*range(SIDE, PARTS), *range(SIDE)]:
             x_copy(0, h).start()
 
     pl.when(x == 1)(across)
@@ -131,12 +135,14 @@
     bias_load.start()
 
     def over_x(s, h, sign):
-        if s > 0:
-            x_copy(sign * (s + 1), h).start()
+        if s == 0:
+            x_copy(sign, h).start()
         else:
-            @pl.when((h < SIDE) | (toward != sign))
+            end = z + s + 1 == Z - 1 if sign > 0 else z - s - 1 == 0
+
+            @pl.when((h < SIDE) | jnp.logical_not(end))
             def _():
-                x_copy(sign, h).start()
+                x_copy(sign * (s + 1), h).start()
 
     def from_above(s, h):
         @pl.when(z < Z - 1 - s)
@@ -155,14 +161,19 @@
             over_x(s, h, -1)
 
     def forward(s, h):
-        pl.when(z < Z // 2)(lambda: from_below(s, h))
         from_above(s, h)
-        pl.when(z >= Z // 2)(lambda: from_below(s, h))
-
-    def sides():
-        x_arrived(0)
-        for h in range(SIDE, PARTS):
-            side_copy(h).start()
+        from_below(s, h)
+
+    def pass_sides():
+        @pl.when((z > 0) & (z < Z - 2))
+        def _():
+            side_down(dom).wait_recv()
+            side_down(dom - 2).start()
+
+        @pl.when((z > 1) & (z < Z - 1))
+        def _():
+            side_up(dom).wait_recv()
+            side_up(dom + 2).start()
 
     for copy in local[0:3]:
         copy.wait()
@@ -217,26 +228,29 @@
         for h in range(PARTS):
             up_copy(k - 1, h).start()
 
-    for k in reversed(line):
-        pl.when(inner & (z + k < Z))(functools.partial(own_up, k))
     for k in line:
-        pl.when(z == 0)(functools.partial(own_up, k))
+        pl.when(z + k < Z)(functools.partial(own_up, k))
 
     units = nb // (4 * GROUP)
     early = units - PARTS * (-(-units // (2 * PARTS)))
     late = units - early
     lax.fori_loop(0, early, build_pair, 0)
-    for h in range(SIDE):
-        pl.when(z == 0)(functools.partial(from_above, 0, h))
-        pl.when(z == Z - 1)(functools.partial(from_below, 0, h))
+    x_arrived(0, SIDE, PARTS - SIDE)
+    pl.when(z == 0)(lambda: side_up(dom + 4).start())
+
+    @pl.when(z == Z - 1)
+    def _():
+        side_down(dom - 4).start()
+        own_down(0)
 
     def slot(h, carry):
         carry = lax.fori_loop(early + late * h // PARTS, early + late * (h + 1) // PARTS, build_pair, carry)
-        forward(1, h)
+        pl.when(inner & (lower | (h < SIDE)))(lambda: from_below(0, h))
+        pl.when(inner)(lambda: forward(1, h))
+        pl.when(outer)(lambda: forward(0, h))
         return carry
 
     lax.fori_loop(0, PARTS, slot, 0)
-    sides()
 
     def self_weights():
         for hi in range(n_hi):
@@ -258,20 +272,19 @@
 
     def add_x(step):
         def work():
-            x_arrived(step)
+            end = z + step == (Z - 1 if step > 0 else 0)
+            pl.when(end)(lambda: x_arrived(step, 0, SIDE))
+            pl.when(jnp.logical_not(end))(lambda: x_arrived(step, 0, PARTS))
+            pl.when(end & (z == 0))(lambda: side_down(dom).wait_recv())
+            pl.when(end & (z == Z - 1))(lambda: side_up(dom).wait_recv())
             add(other + 2 * step, 0, PARTS)
         if_there(step, work)
 
-    def add_pair():
-        x_arrived(toward, SIDE)
-        block_copy(other + 2 * toward, SIDE, PARTS - SIDE, False, side_send, side_recv, dom).wait_recv()
-        add(other + 2 * toward, 0, PARTS)
-
-    def add_next():
+    def add_next(step):
         def work():
-            x_arrived(-toward)
-            add(other - 2 * toward, 0, PARTS)
-        pl.when((z - toward >= 0) & (z - toward < Z))(work)
+            x_arrived(step, 0, PARTS)
+            add(other + 2 * step, 0, PARTS)
+        if_there(step, work)
 
     def both_ways(work, s):
         work(-s)
@@ -280,39 +293,53 @@
     def first_dots():
         local[3].wait()
         acc[...] = jnp.dot(weights[:, mine], gathered[mine, :], preferred_element_type=jnp.float32)
+        x_arrived(0, 0, SIDE)
         add(other, 0, PARTS)
 
-    todo = [self_weights, first_dots, functools.partial(both_ways, add_z, 2)]
+    near, far = jnp.where(outer, 1, 2), jnp.where(outer, 2, 1)
+    self_weights()
+    first_dots()
+    both_ways(add_z, near)
+    pass_sides()
+    first, final = z == 0, z == Z - 1
     for h in range(PARTS):
-        if h < len(todo):
-            todo[h]()
-        if h < SIDE:
-            pl.when(inner)(functools.partial(forward, 0, h))
-        else:
-            forward(0, h)
+        pl.when(inner)(functools.partial(from_above, 0, h))
+        if h >= SIDE:
+            pl.when(inner & upper)(functools.partial(from_below, 0, h))
+    for s, h in ((1, 0), (1, 1), (2, 0), (1, 2), (2, 1), (1, 3)):
+        pl.when(first)(functools.partial(from_above, s, h))
+    for s, h in ((1, 0), (1, 1), (2, 0), (1, 2), (2, 1), (1, 3)):
+        pl.when(final)(functools.partial(from_below, s, h))
+    for h in range(SIDE, PARTS):
+        pl.when(outer)(functools.partial(forward, 2, h))
     for s in range(2, Z - 1):
-        todo = [functools.partial(both_ways, add_z, 1)] if s == 2 else [functools.partial(both_ways, add_z, s)]
         for h in range(PARTS):
-            if h < len(todo):
-                todo[h]()
-            forward(s, h)
-    both_ways(add_z, Z - 1)
-    both_ways(add_x, 2)
-    add_pair()
-    add_next()
+            if s < Z - 2:
+                pl.when(inner)(functools.partial(forward, s, h))
+            if s > 2:
+                pl.when(outer)(functools.partial(forward, s, h))
+    for s in range(3, Z):
+        both_ways(add_z, s)
+    both_ways(add_z, far)
+    add_next(jnp.where(outer, inward, -inward))
+    pl.when(inner)(functools.partial(both_ways, add_x, 2))
     for s in range(3, Z):
         both_ways(add_x, s)
+    add_next(jnp.where(outer, 2 * inward, inward))
 
     pltpu.make_async_copy(w_all, w_all, local_sem.at[4]).wait()
     bias_load.wait()
     pl.when(feat < F - 1)(lambda: pl.semaphore_wait(ready_feat, F - 1 - feat))
-    both[:, 0:FC] = acc[0:nb, :].astype(jnp.bfloat16)
-    both[:, FC:2 * FC] = (acc[nb:2 * nb, :] * inverse).astype(jnp.bfloat16)
     tall = nb // CHUNKS
     short = tall // PIECES
 
     def chunk(r):
         return pl.ds(r * tall, tall)
+
+    def combine(r):
+        at = slice(r * tall, (r + 1) * tall)
+        both[at, 0:FC] = acc[at, :].astype(jnp.bfloat16)
+        both[at, FC:2 * FC] = (acc[nb + r * tall:nb + (r + 1) * tall, :] * inverse[at]).astype(jnp.bfloat16)
 
     def project(r, yy, cc):
         cols = pl.ds(pl.multiple_of((yy * 2 + cc) * share, share), share)
@@ -348,6 +375,8 @@
     for k in range(H):
         yy = lax.rem(y + k + 1, H)
         for r in range(CHUNKS):
+            if k == 0:
+                combine(r)
             send_a[k, chunk(r)] = project(r, yy, 1 - c)
             a_copy(k, r).start()
         for r in range(CHUNKS):
@@ -364,13 +393,19 @@
     for s in range(Z - 1):
         pl.when((z + s + 1 < Z) if s < 2 else (z < Z - 1) & (z >= s))(lambda: up_copy(s, 0, PARTS).wait_send())
         pl.when((z > s) if s < 2 else (z > 0) & (z + s < Z))(lambda: down_copy(s, 0, PARTS).wait_send())
-    side_copy(SIDE, PARTS - SIDE).wait_send()
-    x_copy(0, 0, PARTS).wait_send()
-    x_copy(toward, 0, SIDE).wait_send()
-    pl.when((z - toward >= 0) & (z - toward < Z))(lambda: x_copy(-toward, 0, PARTS).wait_send())
-    for step in range(2, Z):
-        pl.when(z + step < Z)(lambda: x_copy(step, 0, PARTS).wait_send())
-        pl.when(z >= step)(lambda: x_copy(-step, 0, PARTS).wait_send())
+    pl.when((z == Z - 1) | (z > 0) & (z < Z - 2))(lambda: side_down(dom - 2).wait_send())
+    pl.when((z == 0) | (z > 1) & (z < Z - 1))(lambda: side_up(dom + 2).wait_send())
+
+    def x_sent(step):
+        if abs(step) < 2:
+            x_copy(step, 0, PARTS).wait_send()
+        else:
+            end = z + step == (Z - 1 if step > 0 else 0)
+            pl.when(end)(lambda: x_copy(step, 0, SIDE).wait_send())
+            pl.when(jnp.logical_not(end))(lambda: x_copy(step, 0, PARTS).wait_send())
+
+    for step in range(-(Z - 1), Z):
+        if_there(step, functools.partial(x_sent, step))
 
     for r in range(CHUNKS):
         squares = []
@@ -445,9 +480,9 @@
             pltpu.VMEM((CHUNKS, GROUP, nb // CHUNKS), f32),
             pltpu.VMEM((CHUNKS, F - 1, GROUP, nb // CHUNKS), f32),
             dma((6,)),
-            dma((Z - 1,)), dma((Z - 1,)), dma((Z * PARTS,)), dma((Z,)), dma((Z,)),
+            dma((Z - 1,)), dma((Z - 1,)), dma((Z * PARTS,)), dma((Z,)), dma((Z + 1,)),
             dma, dma((H * CHUNKS,)), dma, dma(((H - 1) * CHUNKS * PIECES,)), dma, dma((CHUNKS,)),
-            dma, dma, flag((2,)), flag, flag,
+            dma((2,)), dma((2,)), flag((2,)), flag, flag,
         ],
         compiler_params=pltpu.CompilerParams(collective_id=0, has_side_effects=True),
     )(items, self_ids.reshape(1, nb), neighbor_ids.T, visit_counts.T, w_self, w_neighbor, bias.reshape(1, out))

time: 29 us -> 27.7 us (0.955)
  the two profiles are of different devices: /device:TPU:0 before, /device:TPU:29 now
where the time goes in v2:
time: 27.7 us; the launch traced here: 27.6 us
  Pallas kernels  26.8 us (97%)
  local copies, waits for them, and re-layouts  0.71 us (3%)
    pallas_call x1, Pallas kernels, shards(): pl.pallas_call(functools.partial(kernel, D, F), out_shape=pltpu.VMEM((nb,...  26.8 us
    unnamed x1, local copies, waits for them, and re-layouts  0.71 us

profile of v2, /device:TPU:29, one launch (start us, length us, event | category | flops | bytes accessed | tf_op | source)
XLA Modules:
  0.0 27.6 jit_solution(9128118753433832959)
XLA Ops:
  0.0 26.8 %shard_map.73 = f32[256,256]{1,0:T(8,128)S(1)} custom-call(bf16[256,256]{1,0:T(8,128)(2,1)} %items_hbm.1, s32[1,256]{1,0:T(1,128)} %bitcast.7, s32[50,256]{1,0:T(8,128)} %bitcast.4, s32[50,256]{1,0:T(8,128)} %bitcast.5, bf16[256,1024]{1,0:T(8,128)(2,1)} %ws_hbm.1, bf16[256,1024]{1,0:T(8,128)(2,1)} %wn_hbm.1, f32[1,1024]{1,0:T(1,128)} %bitcast.6), custom_call_target="tpu_custom_call" | custom-call | tf_op jit(solution)/shard_map/pallas_call | solution.py:456
  26.9 0.7 %copy.9 = f32[256,256]{1,0:T(8,128)} copy(f32[256,256]{1,0:T(8,128)S(1)} %shard_map.73) | data formatting | bytes 524288

commit v3 on v2

--- a/solution.py
+++ b/solution.py
@@ -111,13 +111,18 @@
 
     inner, outer = (z > 0) & (z < Z - 1), (z == 0) | (z == Z - 1)
 
-    def own_down(s):
-        for h in range(PARTS):
+    def own_down(s, low=0, high=PARTS):
+        for h in range(low, high):
             down_copy(s, h).start()
 
     for k in reversed(line):
         pl.when(inner & (z >= k))(functools.partial(own_down, k - 1))
-    pl.when(z == Z - 1)(functools.partial(own_down, line[-1] - 1))
+    @pl.when(z == Z - 1)
+    def _():
+        own_down(1, 0, SIDE)
+        own_down(0)
+        own_down(1, SIDE, PARTS)
+
 
     def across():
         for h in [*range(SIDE, PARTS), *range(SIDE)]:
@@ -241,7 +246,6 @@
     @pl.when(z == Z - 1)
     def _():
         side_down(dom - 4).start()
-        own_down(0)
 
     def slot(h, carry):
         carry = lax.fori_loop(early + late * h // PARTS, early + late * (h + 1) // PARTS, build_pair, carry)
@@ -307,9 +311,13 @@
         if h >= SIDE:
             pl.when(inner & upper)(functools.partial(from_below, 0, h))
     for s, h in ((1, 0), (1, 1), (2, 0), (1, 2), (2, 1), (1, 3)):
-        pl.when(first)(functools.partial(from_above, s, h))
-    for s, h in ((1, 0), (1, 1), (2, 0), (1, 2), (2, 1), (1, 3)):
-        pl.when(final)(functools.partial(from_below, s, h))
+        pl.when(first & (x == 0))(functools.partial(from_above, s, h))
+    for s, h in ((1, 0), (1, 1), (1, 2), (2, 0), (1, 3), (2, 1)):
+        pl.when(first & (x == 1))(functools.partial(from_above, s, h))
+    for s, h in ((2, 0), (1, 0), (1, 1), (2, 1), (1, 2), (1, 3)):
+        pl.when(final & (x == 0))(functools.partial(from_below, s, h))
+    for s, h in ((2, 0), (1, 0), (1, 1), (1, 2), (2, 1), (1, 3)):
+        pl.when(final & (x == 1))(functools.partial(from_below, s, h))
     for h in range(SIDE, PARTS):
         pl.when(outer)(functools.partial(forward, 2, h))
     for s in range(2, Z - 1):

time: 27.7 us -> 27.4 us (0.989)
  Pallas kernels: 26.8 us -> 26.5 us
    pallas_call x1, Pallas kernels: 26.8 us -> 26.5 us  [shards(): pl.pallas_call(functools.partial(kernel, D, F), out_shape=pltpu.VMEM((nb,...]
where the time goes in v3:
time: 27.4 us; the launch traced here: 27.2 us
  Pallas kernels  26.5 us (97%)
  local copies, waits for them, and re-layouts  0.71 us (3%)
    pallas_call x1, Pallas kernels, shards(): pl.pallas_call(functools.partial(kernel, D, F), out_shape=pltpu.VMEM((nb,...  26.5 us
    unnamed x1, local copies, waits for them, and re-layouts  0.71 us

profile of v3, /device:TPU:29, one launch (start us, length us, event | category | flops | bytes accessed | tf_op | source)
XLA Modules:
  0.0 27.2 jit_solution(5601544366894102661)
XLA Ops:
  0.0 26.5 %shard_map.73 = f32[256,256]{1,0:T(8,128)S(1)} custom-call(bf16[256,256]{1,0:T(8,128)(2,1)} %items_hbm.1, s32[1,256]{1,0:T(1,128)} %bitcast.7, s32[50,256]{1,0:T(8,128)} %bitcast.4, s32[50,256]{1,0:T(8,128)} %bitcast.5, bf16[256,1024]{1,0:T(8,128)(2,1)} %ws_hbm.1, bf16[256,1024]{1,0:T(8,128)(2,1)} %wn_hbm.1, f32[1,1024]{1,0:T(1,128)} %bitcast.6), custom_call_target="tpu_custom_call" | custom-call | tf_op jit(solution)/shard_map/pallas_call | solution.py:464
  26.5 0.7 %copy.9 = f32[256,256]{1,0:T(8,128)} copy(f32[256,256]{1,0:T(8,128)S(1)} %shard_map.73) | data formatting | bytes 524288

commit v4 on v3

--- a/solution.py
+++ b/solution.py
@@ -13,7 +13,7 @@
 PARTS = 4
 SIDE = 2
 CHUNKS = 2
-PIECES = 2
+PIECES = 1
 
 
 def kernel(
@@ -228,13 +228,22 @@
         pl.semaphore_wait(ready_x, 1)
         across()
 
-    def own_up(k):
-        pl.semaphore_wait(ready_up.at[k - 1], 1)
-        for h in range(PARTS):
+    def own_up(k, low=0, high=PARTS):
+        if low == 0:
+            pl.semaphore_wait(ready_up.at[k - 1], 1)
+        for h in range(low, high):
             up_copy(k - 1, h).start()
 
     for k in line:
-        pl.when(z + k < Z)(functools.partial(own_up, k))
+        pl.when((z > 0) & (z + k < Z))(functools.partial(own_up, k))
+
+    @pl.when(z == 0)
+    def _():
+        own_up(1, 0, SIDE)
+        own_up(2, 0, SIDE)
+        own_up(1, SIDE, PARTS)
+        own_up(2, SIDE, PARTS)
+
 
     units = nb // (4 * GROUP)
     early = units - PARTS * (-(-units // (2 * PARTS)))

time: 27.4 us -> 27.3 us (level)
  no operation moved by 1% of the time
where the time goes in v4:
time: 27.3 us; the launch traced here: 27.2 us
  Pallas kernels  26.5 us (97%)
  local copies, waits for them, and re-layouts  0.71 us (3%)
    pallas_call x1, Pallas kernels, shards(): pl.pallas_call(functools.partial(kernel, D, F), out_shape=pltpu.VMEM((nb,...  26.5 us
    unnamed x1, local copies, waits for them, and re-layouts  0.71 us

profile of v4, /device:TPU:29, one launch (start us, length us, event | category | flops | bytes accessed | tf_op | source)
XLA Modules:
  0.0 27.2 jit_solution(2745082756796110374)
XLA Ops:
  0.0 26.5 %shard_map.73 = f32[256,256]{1,0:T(8,128)S(1)} custom-call(bf16[256,256]{1,0:T(8,128)(2,1)} %items_hbm.1, s32[1,256]{1,0:T(1,128)} %bitcast.7, s32[50,256]{1,0:T(8,128)} %bitcast.4, s32[50,256]{1,0:T(8,128)} %bitcast.5, bf16[256,1024]{1,0:T(8,128)(2,1)} %ws_hbm.1, bf16[256,1024]{1,0:T(8,128)(2,1)} %wn_hbm.1, f32[1,1024]{1,0:T(1,128)} %bitcast.6), custom_call_target="tpu_custom_call" | custom-call | tf_op jit(solution)/shard_map/pallas_call | solution.py:473
  26.5 0.7 %copy.9 = f32[256,256]{1,0:T(8,128)} copy(f32[256,256]{1,0:T(8,128)S(1)} %shard_map.73) | data formatting | bytes 524288

commit v5 on v4

--- a/solution.py
+++ b/solution.py
@@ -120,8 +120,9 @@
     @pl.when(z == Z - 1)
     def _():
         own_down(1, 0, SIDE)
-        own_down(0)
+        own_down(0, 0, SIDE)
         own_down(1, SIDE, PARTS)
+        own_down(0, SIDE, PARTS)
 
 
     def across():

time: 27.3 us -> 27.3 us (level)
  no operation moved by 1% of the time
where the time goes in v5:
time: 27.3 us; the launch traced here: 27.2 us
  Pallas kernels  26.5 us (97%)
  local copies, waits for them, and re-layouts  0.71 us (3%)
    pallas_call x1, Pallas kernels, shards(): pl.pallas_call(functools.partial(kernel, D, F), out_shape=pltpu.VMEM((nb,...  26.5 us
    unnamed x1, local copies, waits for them, and re-layouts  0.71 us

profile of v5, /device:TPU:29, one launch (start us, length us, event | category | flops | bytes accessed | tf_op | source)
XLA Modules:
  0.0 27.2 jit_solution(2766209446249056692)
XLA Ops:
  0.0 26.5 %shard_map.73 = f32[256,256]{1,0:T(8,128)S(1)} custom-call(bf16[256,256]{1,0:T(8,128)(2,1)} %items_hbm.1, s32[1,256]{1,0:T(1,128)} %bitcast.7, s32[50,256]{1,0:T(8,128)} %bitcast.4, s32[50,256]{1,0:T(8,128)} %bitcast.5, bf16[256,1024]{1,0:T(8,128)(2,1)} %ws_hbm.1, bf16[256,1024]{1,0:T(8,128)(2,1)} %wn_hbm.1, f32[1,1024]{1,0:T(1,128)} %bitcast.6), custom_call_target="tpu_custom_call" | custom-call | tf_op jit(solution)/shard_map/pallas_call | solution.py:474
  26.5 0.7 %copy.9 = f32[256,256]{1,0:T(8,128)} copy(f32[256,256]{1,0:T(8,128)S(1)} %shard_map.73) | data formatting | bytes 524288
